TPU v7x, 32 devices: a whole 2x2x4 slice. The times are simulated.
32 devices in a mesh: gx: 2 (over x), gy: 4 (over y, core), gz: 4 (over z).
Axes of the slice: x: 2, y: 2, z: 4, core: 2. Of those that a mesh axis runs over, the one named last changes fastest.
Arguments:
- tokens: bfloat16 [1024, 4608], P('gx', 'gy'), may hold values from -6 to 6
- base_up_weight: bfloat16 [4608, 18432], P('gy', ('gz', 'gx')), may hold values from -0.09375 to 0.09375
- adapter_down_weight: bfloat16 [64, 16, 4608], P(None, None, 'gy'), may hold values from -0.09375 to 0.09375
- adapter_up_weight: bfloat16 [64, 16, 18432], P('gx', None, 'gz'), may hold values from -1.5 to 1.5
- block_adapter_index: int32 [8], P('gx'), may hold values from 0 to 63
- request_rows: int32 [8], P('gx'), may hold values from 1 to 128
Outputs:
- projected: bfloat16 [1024, 18432], P(('gx', 'gy'), 'gz')
Inputs may be any that keep to these rules, and one draw needn't show every extreme that they name: `request_rows`: live rows of each block.
All inputs are finite; a program needn't handle non-finite values.
Results may differ from a plain program's by a relative error of at most 0.0047.
Values may be sent and summed in bfloat16 or wider, within the bound.
A program may use at most 128 MiB of HBM per device.

v0:
```python
import jax
import jax.numpy as jnp
from jax import lax
from jax.sharding import PartitionSpec as P

ADAPTER_COUNT = 64
BLOCK = 128


def body(
    tokens,
    base_up_weight,
    adapter_down_weight,
    adapter_up_weight,
    block_adapter_index,
    request_rows,
):
    rows, shard_width = tokens.shape
    groups = lax.axis_size("gy")
    blocks = rows // BLOCK
    own_blocks = blocks // groups
    own_rows = own_blocks * BLOCK
    first = lax.axis_index("gy") * own_blocks
    rank_values = adapter_down_weight.shape[1]
    catalog = jnp.arange(ADAPTER_COUNT, dtype=jnp.int32)
    selected_adapters = (block_adapter_index[:, None] == catalog[None, :]).astype(jnp.bfloat16)
    chosen_down = jnp.dot(
        selected_adapters,
        adapter_down_weight.reshape(ADAPTER_COUNT, rank_values * shard_width),
        preferred_element_type=jnp.float32,
    )
    chosen_down = chosen_down.astype(jnp.bfloat16).reshape(blocks, rank_values, shard_width)
    tok_blocks = tokens.reshape(blocks, BLOCK, shard_width)
    shrink_part = jnp.einsum(
        "bmd,brd->bmr", tok_blocks, chosen_down, preferred_element_type=jnp.float32
    )
    shrink_own = lax.psum_scatter(shrink_part, "gy", scatter_dimension=0, tiled=True)
    shrink_low = shrink_own.astype(jnp.bfloat16)
    adapter_factors = lax.all_gather(adapter_up_weight, "gx", axis=0, tiled=True)
    out_width = adapter_factors.shape[2]
    own_picks = lax.dynamic_slice_in_dim(selected_adapters, first, own_blocks, 0)
    chosen_up = jnp.dot(
        own_picks,
        adapter_factors.reshape(ADAPTER_COUNT, rank_values * out_width),
        preferred_element_type=jnp.float32,
    )
    chosen_up = chosen_up.astype(jnp.bfloat16).reshape(own_blocks, rank_values, out_width)
    expand = jnp.einsum("bmr,brf->bmf", shrink_low, chosen_up, preferred_element_type=jnp.float32)
    expand = expand.reshape(own_rows, out_width)
    partial_value = jnp.dot(
        tokens,
        lax.all_gather(base_up_weight, "gx", axis=1, tiled=True),
        preferred_element_type=jnp.float32,
    )
    extra = 2.0 * expand
    total = lax.psum_scatter(partial_value, "gy", scatter_dimension=0, tiled=True) + extra
    own_live = lax.dynamic_slice_in_dim(request_rows, first, own_blocks, 0)
    live_mask = (jnp.arange(BLOCK, dtype=jnp.int32)[None, :] < own_live[:, None]).reshape(
        own_rows, 1
    )
    return jnp.where(live_mask, total, 0.0).astype(jnp.bfloat16)


def solution(mesh):
    in_specs = (
        P("gx", "gy"),
        P("gy", ("gz", "gx")),
        P(None, None, "gy"),
        P("gx", None, "gz"),
        P("gx"),
        P("gx"),
    )
    out_specs = P(("gx", "gy"), "gz")
    return jax.shard_map(body, mesh=mesh, in_specs=in_specs, out_specs=out_specs, check_vma=False)
```

profile of v0, /device:TPU:0, one launch (start us, length us, event | category | flops | bytes accessed | tf_op | source)
XLA Modules:
  0.0 291.6 jit_solution(12061952175488107319)
XLA Ops:
  7.4 0.0 copy-start
  7.4 0.0 all-gather.3.cloned.1.call-start
  7.4 0.7 all-gather.3.cloned.1.call-update
  8.1 0.0 copy-start.1
  8.1 0.0 all-gather.5.cloned.1.call-start
  8.1 0.7 all-gather.5.cloned.1.call-update
  8.9 0.0 reduce-scatter.5.cloned.1.call-start
  8.9 0.9 copy-done.1
  9.8 0.0 copy-start.2
  9.8 0.5 copy.7
  10.3 0.1 copy-done.2
  10.4 0.5 convolution_convert_fusion
  10.9 0.0 copy-done
  10.9 1.1 convolution_bitcast_fusion
  12.0 0.0 reduce-scatter.5.cloned.1.call-update
  12.0 0.0 reduce-scatter.3.cloned.1.call-start
  12.0 131.4 %all-gather.3.cloned.1.call-done = bf16[1152,4608]{1,0:T(8,128)(2,1)} async-done(((bf16[1152,2304]{1,0:T(8,128)(2,1)}), bf16[1152,4608]{1,0:T(8,128)(2,1)}) %all-gather.3.cloned.1.call-update) | async-done | bytes 10616848 | tf_op jit(solution)/shard_map/all_gather | solution.py:52
  143.4 13.1 %fusion.11 = f32[512,4608]{1,0:T(8,128)} fusion(bf16[512,1152]{1,0:T(8,128)(2,1)S(1)} %copy-done, bf16[1152,4608]{1,0:T(8,128)(2,1)} %all-gather.3.cloned.1.call-done), kind=kOutput, calls=%fused_computation.16 | convolution fusion | flops 5435817984 | bytes 21233664 | tf_op jit(solution)/shard_map/dot_general | solution.py:50
  156.5 0.0 copy-start.3
  156.5 0.0 reduce-scatter.3.cloned.1.call-update
  156.5 0.6 copy-done.3
  157.2 0.6 dynamic_slice.6
  157.8 0.6 iota_compare_fusion.1
  158.4 0.1 iota_compare_fusion
  158.5 104.5 %all-gather.5.cloned.1.call-done = bf16[64,16,4608]{2,1,0:T(8,128)(2,1)} async-done(((bf16[32,16,4608]{2,1,0:T(8,128)(2,1)}), bf16[64,16,4608]{2,1,0:T(8,128)(2,1)}) %all-gather.5.cloned.1.call-update) | async-done | bytes 9437200 | tf_op jit(solution)/shard_map/all_gather | solution.py:39
  263.0 12.7 %copy.9 = bf16[8,8,16,4608]{3,1,2,0:T(8,128)(2,1)} copy(bf16[8,8,16,4608]{3,2,1,0:T(8,128)(2,1)} %bitcast.28) | data formatting | bytes 18874368
  275.7 5.0 %fusion.7 = f32[1,73728]{1,0:T(1,128)S(1)} fusion(bf16[64,73728]{1,0:T(8,128)(2,1)} %bitcast.27, pred[4,64]{1,0:T(4,128)(4,1)S(1)} %iota_compare_fusion, s32[]{:T(128)S(6)} %select_n.8), kind=kOutput, calls=%fused_computation.11 | convolution fusion | flops 9437184 | bytes 9732356 | tf_op jit(solution)/shard_map/dot_general | solution.py:42
  280.7 0.2 reshape.46
  280.9 0.0 reduce-scatter.5.cloned.1.call-done
  281.0 0.0 reduce-scatter.3.cloned.1.call-done
  281.0 3.2 %fusion.2 = bf16[128,4608]{1,0:T(8,128)(2,1)} fusion(f32[128,4608]{1,0:T(8,128)} %reduce-scatter.3.cloned.1.call-done, bf16[16,4608]{1,0:T(8,128)(2,1)S(1)} %reshape.46, pred[128]{0:T(512)(128)(4,1)S(1)} %iota_compare_fusion.1, f32[1,128,16]{1,2,0:T(8,128)} %reduce-scatter.5.cloned.1.call-done), kind=kOutput, calls=%fused_computation.4 | convolution fusion | flops 21235712 | bytes 3694720 | tf_op jit(solution)/shard_map/bmr,brf->bmf/dot_general | solution.py:48
  (1 shorter events, 0.0 us)
Async XLA Ops:
  7.4 3.5 %copy-start = (bf16[512,1152]{1,0:T(8,128)(2,1)S(1)}, bf16[512,1152]{1,0:T(8,128)(2,1)}, u32[]{:S(2)}) copy-start(bf16[512,1152]{1,0:T(8,128)(2,1)} %param.6) | copy-start | bytes 3538948
  7.4 136.0 %all-gather.3.cloned.1.call-start = ((), (), s32[]{:S(2)}) async-start(), calls=%async_computation.2 | async-start | bytes 15925248 | tf_op jit(solution)/shard_map/all_gather | solution.py:52
  8.1 1.7 copy-start.1
  8.1 254.9 %all-gather.5.cloned.1.call-start = ((), (), s32[]{:S(2)}) async-start(), calls=%async_computation.5 | async-start | bytes 14155776 | tf_op jit(solution)/shard_map/all_gather | solution.py:39
  8.9 272.1 %reduce-scatter.5.cloned.1.call-start = ((), (), s32[]{:S(2)}) async-start(), calls=%async_computation.4 | async-start | bytes 40960 | tf_op jit(solution)/shard_map/reduce_scatter | solution.py:37
  9.8 0.7 copy-start.2
  12.0 269.0 %reduce-scatter.3.cloned.1.call-start = ((), (), s32[]{:S(2)}) async-start(), calls=%async_computation.3 | async-start | bytes 11796480 | tf_op jit(solution)/shard_map/reduce_scatter | solution.py:56
  156.5 0.7 copy-start.3
Sparse Core Ops, SparseCore 0:
  9.7 133.6 all-gather.2
  145.0 117.9 all-gather.4
Sparse Core Ops, SparseCore 1:
  12.1 22.2 reduce-scatter.4
  156.6 77.8 reduce-scatter.2
where the time goes:
time: 292 us
  waiting for transfers between devices  237 us (81%)
  matrix products  22.8 us (8%)
  local copies, waits for them, and re-layouts  15.7 us (5%)
  between operations  14.9 us (5%)
    all_gather x1, waiting for transfers between devices, body(): lax.all_gather(base_up_weight, 'gx', axis=1, tiled=True)  131 us
    all_gather x1, waiting for transfers between devices, body(): lax.all_gather(adapter_up_weight, 'gx', axis=0, tiled=True)  105 us
    unnamed x10, local copies, waits for them, and re-layouts  14.9 us
    dot_general x1, matrix products, body(): jnp.dot(tokens, lax.all_gather(base_up_weight, 'gx', axis=1, tiled=True),...  13.1 us
  transfers between devices with their start and end apart: 4, of which 2 were waited for; matrix products, arithmetic and copies ran while one was open for 12% of the time, Pallas kernels for 0%

commit v1 on v0

v1 whole, which is shorter than its diff:
```python
import functools

import jax
import jax.numpy as jnp
from jax import lax
from jax.experimental import pallas as pl
from jax.experimental.pallas import tpu as pltpu
from jax.sharding import PartitionSpec as P

F32 = jnp.float32
BF16 = jnp.bfloat16
PIECES = 2


def general_body(
    tokens,
    base_up_weight,
    adapter_down_weight,
    adapter_up_weight,
    block_adapter_index,
    request_rows,
):
    rows, shard_width = tokens.shape
    groups = lax.axis_size("gy")
    blocks = block_adapter_index.shape[0]
    block = rows // blocks
    own_blocks = blocks // groups
    own_rows = own_blocks * block
    first = lax.axis_index("gy") * own_blocks
    count, rank_values, _ = adapter_down_weight.shape
    catalog = jnp.arange(count, dtype=jnp.int32)
    selected_adapters = (block_adapter_index[:, None] == catalog[None, :]).astype(BF16)
    chosen_down = jnp.dot(
        selected_adapters,
        adapter_down_weight.reshape(count, rank_values * shard_width),
        preferred_element_type=F32,
    )
    chosen_down = chosen_down.astype(BF16).reshape(blocks, rank_values, shard_width)
    tok_blocks = tokens.reshape(blocks, block, shard_width)
    shrink_part = jnp.einsum("bmd,brd->bmr", tok_blocks, chosen_down, preferred_element_type=F32)
    shrink_own = lax.psum_scatter(shrink_part, "gy", scatter_dimension=0, tiled=True)
    shrink_low = shrink_own.astype(BF16)
    adapter_factors = lax.all_gather(adapter_up_weight, "gx", axis=0, tiled=True)
    out_width = adapter_factors.shape[2]
    own_picks = lax.dynamic_slice_in_dim(selected_adapters, first, own_blocks, 0)
    chosen_up = jnp.dot(
        own_picks,
        adapter_factors.reshape(count, rank_values * out_width),
        preferred_element_type=F32,
    )
    chosen_up = chosen_up.astype(BF16).reshape(own_blocks, rank_values, out_width)
    expand = jnp.einsum("bmr,brf->bmf", shrink_low, chosen_up, preferred_element_type=F32)
    expand = expand.reshape(own_rows, out_width)
    partial_value = jnp.dot(
        tokens,
        lax.all_gather(base_up_weight, "gx", axis=1, tiled=True),
        preferred_element_type=F32,
    )
    extra = 2.0 * expand
    total = lax.psum_scatter(partial_value, "gy", scatter_dimension=0, tiled=True) + extra
    own_live = lax.dynamic_slice_in_dim(request_rows, first, own_blocks, 0)
    live_mask = (jnp.arange(block, dtype=jnp.int32)[None, :] < own_live[:, None]).reshape(
        own_rows, 1
    )
    return jnp.where(live_mask, total, 0.0).astype(BF16)


def kernel(
    chunks,
    index_ref,
    live_ref,
    tok_hbm,
    w_hbm,
    down_hbm,
    up_hbm,
    out_ref,
    tok,
    far_tok,
    w,
    down,
    up,
    pick,
    pick_in,
    up_own,
    up_send,
    up_in,
    shrink_own,
    shrink_send,
    shrink_in,
    a_send,
    a_in,
    keep,
    b_send,
    b_in,
    c_send,
    c_in,
    local_sem,
    a_sem,
    b_sem,
    c_sem,
    x_sem,
    z_sem,
    pick_sem,
    up_sem,
    shrink_sem,
):
    gx = lax.axis_index("gx")
    gy = lax.axis_index("gy")
    gz = lax.axis_index("gz")
    core = lax.rem(gy, 2)
    yy = lax.div(gy, 2)
    y_far = 1 - yy
    zp = lax.rem(gz, 2)
    x_peer = {"gx": 1 - gx}
    core_peer = {"gy": gy + 1 - 2 * core}
    y_peer = {"gy": lax.rem(gy + 2, 4)}
    diagonal = {"gy": 3 - gy}
    z_peer = {"gz": gz + 1 - 2 * zp}
    block = out_ref.shape[0]
    cols = w.shape[1]
    wide = cols // chunks
    ranks = down.shape[1]
    held = up.shape[0]
    piece = block // PIECES

    def remote(src, dst, sems, n, device):
        return pltpu.make_async_remote_copy(
            src_ref=src,
            dst_ref=dst,
            send_sem=sems.at[0, n],
            recv_sem=sems.at[1, n],
            device_id=device,
            device_id_type=pl.DeviceIdType.MESH,
        )

    tok_load = pltpu.make_async_copy(tok_hbm, tok, local_sem.at[0])
    tok_load.start()
    w_loads = []
    for n in range(chunks):
        span = pl.ds(n * wide, wide)
        load = pltpu.make_async_copy(w_hbm.at[:, span], w.at[:, span], local_sem.at[3 + n])
        load.start()
        w_loads.append(load)
    down_load = pltpu.make_async_copy(down_hbm, down, local_sem.at[1])
    down_load.start()
    up_load = pltpu.make_async_copy(up_hbm, up, local_sem.at[2])
    up_load.start()

    barrier = pltpu.get_barrier_semaphore()
    for device in (x_peer, core_peer, y_peer, diagonal, z_peer):
        pl.semaphore_signal(
            barrier, inc=1, device_id=device, device_id_type=pl.DeviceIdType.MESH
        )

    wanted = index_ref[gy]
    rank_at = lax.broadcasted_iota(jnp.int32, (ranks, held), 0)
    slot_at = lax.broadcasted_iota(jnp.int32, (ranks, held), 1)
    for half in range(2):
        hit = slot_at + half * held == wanted * ranks + rank_at
        pick[half] = jnp.where(hit, 1.0, 0.0).astype(BF16)

    pl.semaphore_wait(barrier, 5)
    tok_load.wait()

    x_copies, z_copies = [], []
    for u, y_at in enumerate((y_far, yy)):
        for q in range(PIECES):
            at = pl.multiple_of((2 * y_at + zp) * block + q * piece, piece)
            n = u * PIECES + q
            span = pl.ds(at, piece)
            copy = remote(tok.at[span, :], far_tok.at[span, :], x_sem, n, x_peer)
            copy.start()
            x_copies.append(copy)
            z_copies.append(remote(far_tok.at[span, :], far_tok.at[span, :], z_sem, n, z_peer))
    pick_copy = remote(pick.at[1 - gx], pick_in, pick_sem, 0, x_peer)
    pick_copy.start()

    def row(c):
        return pl.ds(pl.multiple_of(c * block, block), block)

    a_copies, b_copies, c_copies = {}, {}, {}

    def multiply(tokens_ref, g, u, y_at, n):
        s = (g * 2 + u) * chunks + n
        lhs = tokens_ref[pl.ds(pl.multiple_of(y_at * 2 * block, 2 * block), 2 * block), :]
        part = jnp.dot(lhs, w[:, n * wide : (n + 1) * wide], preferred_element_type=F32)
        low, high = part[:block], part[block:]
        mine = core == 0
        a_send[s] = jnp.where(mine, high, low)
        keep[s] = jnp.where(mine, low, high)
        copy = remote(a_send.at[s], a_in.at[s], a_sem, s, core_peer)
        copy.start()
        a_copies[s] = copy

    def pair_up(g, u, n):
        s = (g * 2 + u) * chunks + n
        a_copies[s].wait_recv()
        both = keep[s] + a_in[s]
        if u == 0:
            k = g * chunks + n
            b_send[k] = both.astype(BF16)
            copy = remote(b_send.at[k], b_in.at[k], b_sem, k, y_peer)
            copy.start()
            b_copies[k] = copy
        else:
            keep[s] = both

    def relay(n):
        x_copies[n].wait_recv()
        z_copies[n].start()

    waiting = None
    for u, y_at in enumerate((y_far, yy)):
        for n in range(chunks):
            if u == 0:
                w_loads[n].wait()
            multiply(tok, 0, u, y_at, n)
            if waiting is not None:
                pair_up(*waiting)
            waiting = (0, u, n)
    pair_up(*waiting)

    relay(0)
    down_load.wait()
    shrink_copies = []
    for d, (device, at) in enumerate(
        (
            (core_peer, core_peer["gy"]),
            (y_peer, y_peer["gy"]),
            (diagonal, diagonal["gy"]),
            (None, gy),
        )
    ):
        value = lax.dot_general(
            down[index_ref[at]],
            tok[row(at), :],
            (((1,), (1,)), ((), ())),
            preferred_element_type=F32,
        )
        if device is None:
            shrink_own[...] = value
        else:
            shrink_send[d] = value
            copy = remote(shrink_send.at[d], shrink_in.at[d], shrink_sem, d, device)
            copy.start()
            shrink_copies.append(copy)
    relay(1)
    pick_copy.wait_recv()
    up_load.wait()
    up_width = up.shape[1]
    for n in range(2 * chunks):
        span = slice(n * wide, (n + 1) * wide)
        up_own[:, span] = jnp.dot(
            pick[gx], up[:, span], preferred_element_type=F32
        ).astype(BF16)
        up_send[:, span] = jnp.dot(
            pick_in[...], up[:, span], preferred_element_type=F32
        ).astype(BF16)
    up_copy = remote(up_send, up_in, up_sem, 0, x_peer)
    up_copy.start()

    relay(2)
    for n in range(PIECES):
        z_copies[n].wait_recv()
    waiting = None
    for n in range(chunks):
        multiply(far_tok, 1, 0, y_far, n)
        if waiting is not None:
            pair_up(*waiting)
        waiting = (1, 0, n)
    pair_up(*waiting)
    for n in range(3, 2 * PIECES):
        relay(n)
    for n in range(PIECES, 2 * PIECES):
        z_copies[n].wait_recv()
    waiting = None
    for n in range(chunks):
        multiply(far_tok, 1, 1, yy, n)
        if waiting is not None:
            pair_up(*waiting)
        waiting = (1, 1, n)
    pair_up(*waiting)

    for copy in shrink_copies:
        copy.wait_recv()
    shrink = (shrink_own[...] + shrink_in[0]) + (shrink_in[1] + shrink_in[2])
    shrink_low = shrink.astype(BF16)
    up_copy.wait_recv()
    live = lax.broadcasted_iota(jnp.int32, (block, 1), 0) < live_ref[gy]

    def finish(side, n, base):
        span = pl.ds(pl.multiple_of(side * cols + n * wide, 128), wide)
        factor = up_own[:, span] + up_in[:, span]
        expand = lax.dot_general(
            shrink_low, factor, (((0,), (0,)), ((), ())), preferred_element_type=F32
        )
        out_ref[:, span] = jnp.where(live, base + 2.0 * expand, 0.0).astype(BF16)

    for n in range(chunks):
        b_copies[n].wait_recv()
        finish(gx, n, keep[chunks + n] + b_in[n].astype(F32))
    for n in range(chunks):
        k = chunks + n
        b_copies[k].wait_recv()
        c_send[n] = (keep[3 * chunks + n] + b_in[k].astype(F32)).astype(BF16)
        copy = remote(c_send.at[n], c_in.at[n], c_sem, n, x_peer)
        copy.start()
        c_copies[n] = copy
    for n in range(chunks):
        c_copies[n].wait_recv()
        finish(1 - gx, n, c_in[n].astype(F32))

    for copy in (
        x_copies
        + z_copies
        + [pick_copy, up_copy]
        + shrink_copies
        + list(a_copies.values())
        + list(b_copies.values())
        + list(c_copies.values())
    ):
        copy.wait_send()


def fused_body(
    tokens,
    base_up_weight,
    adapter_down_weight,
    adapter_up_weight,
    block_adapter_index,
    request_rows,
):
    rows, depth = tokens.shape
    cols = base_up_weight.shape[1]
    block = rows // block_adapter_index.shape[0]
    count, ranks, _ = adapter_down_weight.shape
    held_count, _, out_width = adapter_up_weight.shape
    held = held_count * ranks
    chunks = cols // max(n for n in range(256, 769, 256) if cols % n == 0)
    wide = cols // chunks
    steps = 4 * chunks
    anywhere = pl.BlockSpec(memory_space=pl.ANY)
    smem = pl.BlockSpec(memory_space=pltpu.SMEM)

    def dma(n):
        return pltpu.SemaphoreType.DMA((2, n))

    return pl.pallas_call(
        functools.partial(kernel, chunks),
        out_shape=jax.ShapeDtypeStruct((block, out_width), BF16),
        in_specs=[smem, smem, anywhere, anywhere, anywhere, anywhere],
        out_specs=pl.BlockSpec(memory_space=pltpu.VMEM),
        scratch_shapes=[
            pltpu.VMEM((rows, depth), BF16),
            pltpu.VMEM((rows, depth), BF16),
            pltpu.VMEM((depth, cols), BF16),
            pltpu.VMEM((count, ranks, depth), BF16),
            pltpu.VMEM((held, out_width), BF16),
            pltpu.VMEM((2, ranks, held), BF16),
            pltpu.VMEM((ranks, held), BF16),
            pltpu.VMEM((ranks, out_width), BF16),
            pltpu.VMEM((ranks, out_width), BF16),
            pltpu.VMEM((ranks, out_width), BF16),
            pltpu.VMEM((ranks, block), F32),
            pltpu.VMEM((3, ranks, block), F32),
            pltpu.VMEM((3, ranks, block), F32),
            pltpu.VMEM((steps, block, wide), F32),
            pltpu.VMEM((steps, block, wide), F32),
            pltpu.VMEM((steps, block, wide), F32),
            pltpu.VMEM((2 * chunks, block, wide), BF16),
            pltpu.VMEM((2 * chunks, block, wide), BF16),
            pltpu.VMEM((chunks, block, wide), BF16),
            pltpu.VMEM((chunks, block, wide), BF16),
            pltpu.SemaphoreType.DMA((3 + chunks,)),
            dma(steps),
            dma(2 * chunks),
            dma(chunks),
            dma(2 * PIECES),
            dma(2 * PIECES),
            dma(1),
            dma(1),
            dma(3),
        ],
        compiler_params=pltpu.CompilerParams(
            collective_id=0, has_side_effects=True, vmem_limit_bytes=60 * 1024 * 1024
        ),
    )(
        block_adapter_index,
        request_rows,
        tokens,
        base_up_weight,
        adapter_down_weight,
        adapter_up_weight.reshape(held, out_width),
    )


def solution(mesh):
    in_specs = (
        P("gx", "gy"),
        P("gy", ("gz", "gx")),
        P(None, None, "gy"),
        P("gx", None, "gz"),
        P("gx"),
        P("gx"),
    )
    out_specs = P(("gx", "gy"), "gz")
    sizes = mesh.shape

    def body(*arrays):
        blocks = arrays[4].shape[0]
        paired = sizes["gx"] == 2 and sizes["gy"] == 4 and sizes["gz"] % 2 == 0
        if paired and blocks == sizes["gy"]:
            return fused_body(*arrays)
        return general_body(*arrays)

    return jax.shard_map(body, mesh=mesh, in_specs=in_specs, out_specs=out_specs, check_vma=False)
```

time: 292 us -> 54.6 us (0.19)
  waiting for transfers between devices: 237 us -> 0 us
  Pallas kernels: 0 us -> 52.1 us
  matrix products: 22.8 us -> 0 us
  between operations: 14.9 us -> 0.01 us
  local copies, waits for them, and re-layouts: 15.7 us -> 2.36 us
    all_gather x2 -> x0, waiting for transfers between devices: 236 us -> none  [the longest x1 131 us: body(): lax.all_gather(base_up_weight, 'gx', axis=1, tiled=True)]
    pallas_call x0 -> x1, Pallas kernels: none -> 52.1 us  [fused_body(): pl.pallas_call(functools.partial(kernel, chunks), out_shape=jax.ShapeDtyp...]
    dot_general x5 -> x0, matrix products: 22.8 us -> none  [the longest x1 13.1 us: body(): jnp.dot(tokens, lax.all_gather(base_up_weight, 'gx', axis=1, tiled=True),...]
    unnamed x10 -> x1, local copies, waits for them, and re-layouts: 14.9 us -> 2.36 us
  transfers between devices with their start and end apart: 4 -> 0, of which waited for: 2 -> 0; matrix products, arithmetic and copies ran while one was open for 12% -> 0% of each run, Pallas kernels for 0% -> 0%
where the time goes in v1:
time: 54.6 us; the launch traced here: 54.5 us
  Pallas kernels  52.1 us (95%)
  local copies, waits for them, and re-layouts  2.36 us (4%)
    pallas_call x1, Pallas kernels, fused_body(): pl.pallas_call(functools.partial(kernel, chunks), out_shape=jax.ShapeDtyp...  52.1 us
    unnamed x1, local copies, waits for them, and re-layouts  2.36 us

profile of v1, /device:TPU:0, one launch (start us, length us, event | category | flops | bytes accessed | tf_op | source)
XLA Modules:
  0.0 54.5 jit_solution(16270153681327964373)
XLA Ops:
  0.0 52.1 %shard_map.64 = bf16[128,4608]{1,0:T(8,128)(2,1)} custom-call(s32[4]{0:T(128)} %index_ref.1, s32[4]{0:T(128)} %live_ref.1, bf16[512,1152]{1,0:T(8,128)(2,1)} %tok_hbm.1, bf16[1152,2304]{1,0:T(8,128)(2,1)} %w_hbm.1, bf16[64,16,1152]{2,1,0:T(8,128)(2,1)} %down_hbm.1, bf16[512,4608]{1,0:T(8,128)(2,1)} %bitcast.1), custom_call_target="tpu_custom_call" | custom-call | tf_op jit(solution)/shard_map/pallas_call | solution.py:348
  52.1 2.4 %copy.8 = bf16[128,4608]{1,0:T(8,128)(2,1)} copy(bf16[128,4608]{1,0:T(8,128)(2,1)} %shard_map.64) | data formatting | bytes 2359296

commit v2 on v1

--- a/solution.py
+++ b/solution.py
@@ -9,7 +9,7 @@
 
 F32 = jnp.float32
 BF16 = jnp.bfloat16
-PIECES = 2
+PIECES = 1
 
 
 def general_body(
@@ -244,7 +244,6 @@
             copy = remote(shrink_send.at[d], shrink_in.at[d], shrink_sem, d, device)
             copy.start()
             shrink_copies.append(copy)
-    relay(1)
     pick_copy.wait_recv()
     up_load.wait()
     up_width = up.shape[1]
@@ -259,7 +258,7 @@
     up_copy = remote(up_send, up_in, up_sem, 0, x_peer)
     up_copy.start()
 
-    relay(2)
+    relay(1)
     for n in range(PIECES):
         z_copies[n].wait_recv()
     waiting = None
@@ -269,7 +268,7 @@
             pair_up(*waiting)
         waiting = (1, 0, n)
     pair_up(*waiting)
-    for n in range(3, 2 * PIECES):
+    for n in range(2, 2 * PIECES):
         relay(n)
     for n in range(PIECES, 2 * PIECES):
         z_copies[n].wait_recv()
@@ -336,7 +335,7 @@
     count, ranks, _ = adapter_down_weight.shape
     held_count, _, out_width = adapter_up_weight.shape
     held = held_count * ranks
-    chunks = cols // max(n for n in range(256, 769, 256) if cols % n == 0)
+    chunks = cols // max(n for n in range(128, 1153, 128) if cols % n == 0)
     wide = cols // chunks
     steps = 4 * chunks
     anywhere = pl.BlockSpec(memory_space=pl.ANY)

time: 54.6 us -> 50.8 us (0.930)
  Pallas kernels: 52.1 us -> 48.3 us
    pallas_call x1, Pallas kernels: 52.1 us -> 48.3 us  [fused_body(): pl.pallas_call(functools.partial(kernel, chunks), out_shape=jax.ShapeDtyp...]
where the time goes in v2:
time: 50.8 us; the launch traced here: 50.7 us
  Pallas kernels  48.3 us (95%)
  local copies, waits for them, and re-layouts  2.36 us (5%)
    pallas_call x1, Pallas kernels, fused_body(): pl.pallas_call(functools.partial(kernel, chunks), out_shape=jax.ShapeDtyp...  48.3 us
    unnamed x1, local copies, waits for them, and re-layouts  2.36 us

profile of v2, /device:TPU:0, one launch (start us, length us, event | category | flops | bytes accessed | tf_op | source)
XLA Modules:
  0.0 50.7 jit_solution(2586818606957683466)
XLA Ops:
  0.0 48.3 %shard_map.64 = bf16[128,4608]{1,0:T(8,128)(2,1)} custom-call(s32[4]{0:T(128)} %index_ref.1, s32[4]{0:T(128)} %live_ref.1, bf16[512,1152]{1,0:T(8,128)(2,1)} %tok_hbm.1, bf16[1152,2304]{1,0:T(8,128)(2,1)} %w_hbm.1, bf16[64,16,1152]{2,1,0:T(8,128)(2,1)} %down_hbm.1, bf16[512,4608]{1,0:T(8,128)(2,1)} %bitcast.1), custom_call_target="tpu_custom_call" | custom-call | tf_op jit(solution)/shard_map/pallas_call | solution.py:347
  48.3 2.4 %copy.8 = bf16[128,4608]{1,0:T(8,128)(2,1)} copy(bf16[128,4608]{1,0:T(8,128)(2,1)} %shard_map.64) | data formatting | bytes 2359296
